TPU v7x, 32 devices: a whole 2x2x4 slice. The times are simulated.
32 devices in a mesh: lat: 8 (over z, x), lon: 4 (over y, core).
Axes of the slice: x: 2, y: 2, z: 4, core: 2. Of those that a mesh axis runs over, the one named last changes fastest.
Arguments:
- increment: bfloat16 [16, 8, 144, 128], P('lat', 'lon'), may hold values from -6 to 6
- cotangent: bfloat16 [8, 4, 40, 144, 128], P('lat', 'lon'), may hold values from -6 to 6
- weights: bfloat16 [8, 4, 40, 16, 128, 128], P('lat', 'lon'), may hold values from -0.1875 to 0.1875
- source_ids: int32 [8, 4, 40, 16], P('lat', 'lon'), may hold values from 0 to 127, as said below
- counts: int32 [8, 4, 40], P('lat', 'lon'), may hold values from 0 to 16, as said below
Outputs:
- ocean: bfloat16 [8, 4, 40, 144, 128], P('lat', 'lon')
- atmos_adjoint: bfloat16 [16, 8, 144, 128], P('lat', 'lon')
Inputs may be any that keep to these rules, and one draw needn't show every extreme that they name: source_ids[i, j, t, k] = a * 8 + b with block row a between i * 2 - 1 and (i + 1) * 2, and block column b equal, modulo 8, to one of j * 2 - 1 to (j + 1) * 2. `counts`: every device's tile (i, j) has some target block with exactly 16 live slots.
All inputs are finite; a program needn't handle non-finite values.
Results may differ from a plain program's by a relative error of at most 0.001.
Values may be sent and summed in bfloat16 or wider, within the bound.
A program may use at most 192 MiB of HBM per device.

v0:
```python
import jax
import jax.numpy as jnp
from jax import lax
from jax.sharding import PartitionSpec as P


def from_behind(value, axis, by):
    peers = lax.axis_size(axis)
    return lax.ppermute(value, axis, [(i, (i + by) % peers) for i in range(peers)])


def passed_along(block, axis, distance):
    devices = range(lax.axis_size(axis))
    route = [(i - distance, i) for i in devices if i - distance in devices]
    return lax.ppermute(block, axis, route)


def with_halo(block, sides, width):
    for axis, dim in sides:
        count = lax.axis_size(axis)
        forward = [(i, i + 1) for i in range(count - 1)]
        forward.append((count - 1, 0))
        backward = [(target, source) for source, target in forward]
        low = lax.ppermute(
            lax.slice_in_dim(block, block.shape[dim] - width, None, axis=dim), axis, forward
        )
        high = lax.ppermute(lax.slice_in_dim(block, 0, width, axis=dim), axis, backward)
        block = jnp.concatenate([low, block, high], axis=dim)
    return block


def fold_lon(partial_value):
    from_west = from_behind(partial_value[:, -1:], "lon", 1)
    from_east = from_behind(partial_value[:, :1], "lon", -1)
    middle = partial_value[:, 1:-1]
    return middle.at[:, :1].add(from_west).at[:, -1:].add(from_east)


def fold_lat(partial_value):
    from_north = passed_along(partial_value[-1:], "lat", 1)
    from_south = passed_along(partial_value[:1], "lat", -1)
    middle = partial_value[1:-1]
    return middle.at[:1].add(from_north).at[-1:].add(from_south)


def body(increment, cotangent, weights, source_ids, counts):
    tile_side = increment.shape[0]
    level_rows = increment.shape[2]
    block_cells = increment.shape[3]
    lon_count = lax.axis_size("lon")
    cycle_blocks = tile_side * lon_count
    lat_index = lax.axis_index("lat")
    lon_index = lax.axis_index("lon")
    source_list = source_ids[0, 0]
    live_counts = counts[0, 0]
    blocks = weights[0, 0]
    cotan_local = cotangent[0, 0]
    slot_count = blocks.shape[1]
    block_row = source_list // cycle_blocks
    block_col = source_list % cycle_blocks
    ext_col = (block_col - lon_index * tile_side + 1 + cycle_blocks) % cycle_blocks
    ext_width = tile_side + 2
    ext_rows = tile_side + 2
    ext_row = block_row - lat_index * tile_side + 1
    ext_total = ext_rows * ext_width
    positions = ext_row * ext_width + ext_col
    slot_index = jnp.arange(slot_count, dtype=jnp.int32)[None, :]
    active = slot_index < live_counts[:, None]
    place_index = jnp.arange(ext_total, dtype=jnp.int32)[None, None, :]
    selector = jnp.logical_and(positions[:, :, None] == place_index, active[:, :, None])
    extended = with_halo(increment, (("lat", 0), ("lon", 1)), 1)
    flattened = extended.reshape(ext_total, level_rows, block_cells)
    picked = jnp.einsum(
        "tke,ews->tkws",
        selector.astype(jnp.bfloat16),
        flattened,
        preferred_element_type=jnp.float32,
    ).astype(jnp.bfloat16)
    ocean_sum = jnp.einsum("tkws,tksb->twb", picked, blocks, preferred_element_type=jnp.float32)
    contribution = jnp.einsum(
        "twb,tksb->tkws", cotan_local, blocks, preferred_element_type=jnp.float32
    )
    partial_value = jnp.einsum(
        "tke,tkws->ews",
        selector.astype(jnp.float32),
        contribution,
        precision=lax.Precision.HIGHEST,
        preferred_element_type=jnp.float32,
    )
    partial_value = partial_value.reshape(ext_rows, ext_width, level_rows, block_cells)
    result_blocks = fold_lat(fold_lon(partial_value))
    return (ocean_sum.astype(jnp.bfloat16)[None, None], result_blocks.astype(jnp.bfloat16))


def solution(mesh):
    placed = (
        P("lat", "lon", None, None),
        P("lat", "lon", None, None, None),
        P("lat", "lon", None, None, None, None),
        P("lat", "lon", None, None),
        P("lat", "lon", None),
    )
    return jax.shard_map(
        body,
        mesh=mesh,
        in_specs=placed,
        out_specs=(P("lat", "lon", None, None, None), P("lat", "lon", None, None)),
        check_vma=False,
    )
```

profile of v0, /device:TPU:8, one launch (start us, length us, event | category | flops | bytes accessed | tf_op | source)
XLA Modules:
  0.0 133.6 jit_solution(1068564448842922185)
XLA Ops:
  0.6 0.0 copy-start
  0.6 1.7 %fusion.41 = (bf16[1,2,144,128]{3,2,1,0:T(8,128)(2,1)}, bf16[1,2,144,128]{3,2,1,0:T(8,128)(2,1)}) fusion(bf16[2,2,144,128]{3,2,1,0:T(8,128)(2,1)} %param.13), kind=kLoop, calls=%fused_computation.57 | loop fusion | bytes 294912 | tf_op jit(solution)/shard_map/slice | solution.py:27
  2.3 1.5 %collective-permute-start = (bf16[1,2,144,128]{3,2,1,0:T(8,128)(2,1)}, bf16[1,2,144,128]{3,2,1,0:T(8,128)(2,1)}, u32[]{:S(2)}, u32[]{:S(2)}) collective-permute-start(bf16[1,2,144,128]{3,2,1,0:T(8,128)(2,1)} %get-tuple-element.58), channel_id=1, source_target_pairs={{0,4},{4,8},{8,12},{12,16},{16,20},{20,24},{24,28},{28,0},{1,5},{5... | collective-permute-start | bytes 221192 | tf_op jit(solution)/shard_map/ppermute | solution.py:24
  3.8 1.4 %collective-permute-start.1 = (bf16[1,2,144,128]{3,2,1,0:T(8,128)(2,1)}, bf16[1,2,144,128]{3,2,1,0:T(8,128)(2,1)S(1)}, u32[]{:S(2)}, u32[]{:S(2)}) collective-permute-start(bf16[1,2,144,128]{3,2,1,0:T(8,128)(2,1)} %get-tuple-element.57), channel_id=1, source_target_pairs={{4,0},{8,4},{12,8},{16,12},{20,16},{24,20},{28,24},{0,28},{5,1},{9... | collective-permute-start | bytes 221192 | tf_op jit(solution)/shard_map/ppermute | solution.py:27
  5.3 0.7 iota_compare_fusion.1
  5.9 0.0 copy-done
  5.9 0.0 copy-start.4
  5.9 23.1 %fusion.4 = f32[40,16,128,144]{2,3,1,0:T(8,128)} fusion(bf16[1,1,40,16,128,128]{5,4,3,2,1,0:T(8,128)(2,1)} %param.15, bf16[1,1,40,144,128]{4,3,2,1,0:T(8,128)(2,1)S(1)} %copy-done), kind=kOutput, calls=%fused_computation.5 | convolution fusion | flops 3019898880 | bytes 69632000 | tf_op jit(solution)/shard_map/twb,tksb->tkws/dot_general | solution.py:80
  29.1 0.0 copy-done.4
  29.1 0.0 copy-start.3
  29.1 0.0 slice-start
  29.1 0.0 slice-start.1
  29.1 0.0 slice-start.2
  29.1 58.1 %fusion = f32[16,144,128,1]{2,0,3,1:T(8,128)S(1)} fusion(f32[40,16,128,144]{2,3,1,0:T(8,128)} %fusion.4, s32[40,16]{0,1:T(8,128)S(1)} %fusion.31, pred[40,16]{0,1:T(8,128)(4,1)S(1)} %iota_compare_fusion.1), kind=kOutput, calls=%fused_computation | convolution fusion | flops 2264944640 | bytes 48368768 | tf_op jit(solution)/shard_map/tke,tkws->ews/dot_general | solution.py:83
  87.3 0.0 collective-permute-done
  87.3 0.9 constant_dynamic-update-slice_fusion.2
  88.2 0.0 copy-done.3
  88.2 0.0 collective-permute-done.1
  88.3 0.1 collective-permute-start.2
  88.3 1.7 %collective-permute-start.3 = (bf16[4,1,144,128]{3,2,1,0:T(8,128)(2,1)S(1)}, bf16[4,1,144,128]{3,2,1,0:T(8,128)(2,1)S(1)}, u32[]{:S(2)}, u32[]{:S(2)}) collective-permute-start(bf16[4,1,144,128]{3,2,1,0:T(8,128)(2,1)S(1)} %get-tuple-element.56), channel_id=1, source_target_pairs={{1,0},{2,1},{3,2},{0,3},{5,4},{6,5},{7,6},{4,7},{9,8},{10,9},{11,1... | collective-permute-start | bytes 442376 | tf_op jit(solution)/shard_map/ppermute | solution.py:27
  90.1 0.6 fusion.38
  90.7 0.0 slice-start.3
  90.7 0.1 collective-permute-start.4
  90.8 1.8 %collective-permute-start.5 = (f32[4,1,144,128]{3,2,1,0:T(8,128)S(1)}, f32[4,1,144,128]{3,2,1,0:T(8,128)S(1)}, u32[]{:S(2)}, u32[]{:S(2)}) collective-permute-start(f32[4,1,144,128]{3,2,1,0:T(8,128)S(1)} %copy.21), channel_id=1, source_target_pairs={{0,3},{1,0},{2,1},{3,2},{4,7},{5,4},{6,5},{7,6},{8,11},{9,8},{10,9... | collective-permute-start | bytes 884744 | tf_op jit(solution)/shard_map/ppermute | solution.py:9
  92.6 0.3 slice.164
  92.9 0.1 copy.18
  93.0 0.0 collective-permute-done.2
  93.0 1.2 collective-permute-done.3
  94.2 0.1 pad_maximum_fusion
  94.3 0.0 slice-start.4
  94.3 10.7 %fusion.13 = bf16[40,16,144,128]{3,0,2,1:T(8,128)(2,1)} fusion(bf16[16,144,128,1]{2,1,0,3:T(8,128)(2,1)S(1)} %bitcast.61, s32[40,16]{0,1:T(8,128)S(1)} %fusion.31, pred[40,16]{0,1:T(8,128)(4,1)S(1)} %iota_compare_fusion.1), kind=kOutput, calls=%fused_computation.12 | convolution fusion | flops 377507840 | bytes 24185984 | tf_op jit(solution)/shard_map/tke,ews->tkws/dot_general | solution.py:73
  105.0 0.0 collective-permute-done.4
  105.1 0.0 collective-permute-done.5
  105.1 0.1 fusion.15
  105.1 0.0 copy-start.2
  105.2 0.8 copy-done.2
  106.0 0.7 fusion.39
  106.7 0.0 copy-start.1
  106.7 2.6 %collective-permute-start.6 = (f32[1,2,144,128]{3,2,1,0:T(8,128)}, f32[1,2,144,128]{3,2,1,0:T(8,128)S(1)}, u32[]{:S(2)}, u32[]{:S(2)}) collective-permute-start(f32[1,2,144,128]{3,2,1,0:T(8,128)} %get-tuple-element.54), channel_id=1, source_target_pairs={{0,4},{4,8},{8,12},{12,16},{16,20},{20,24},{24,28},{1,5},{5,9},{9,... | collective-permute-start | bytes 442376 | tf_op jit(solution)/shard_map/ppermute | solution.py:15
  109.3 0.0 slice-done
  109.3 0.0 slice-done.1
  109.3 0.0 slice-done.2
  109.3 0.0 slice-done.3
  109.3 0.0 slice-done.4
  109.4 13.8 %fusion.10 = bf16[1,1,40,144,128]{4,3,2,1,0:T(8,128)(2,1)} fusion(bf16[1,1,40,16,128,128]{5,4,3,2,1,0:T(8,128)(2,1)S(1)} %bitcast.58, bf16[40,16,144,128]{3,0,2,1:T(8,128)(2,1)} %fusion.13), kind=kOutput, calls=%fused_computation.10 | convolution fusion | flops 3020636160 | bytes 46039040 | tf_op jit(solution)/shard_map/tkws,tksb->twb/dot_general | solution.py:79
  123.2 1.0 slice.169
  124.2 4.2 %collective-permute-start.7 = (f32[1,2,144,128]{3,2,1,0:T(8,128)}, f32[1,2,144,128]{3,2,1,0:T(8,128)S(1)}, u32[]{:S(2)}, u32[]{:S(2)}) collective-permute-start(f32[1,2,144,128]{3,2,1,0:T(8,128)} %get-tuple-element.53), channel_id=1, source_target_pairs={{4,0},{8,4},{12,8},{16,12},{20,16},{24,20},{28,24},{5,1},{9,5},{13... | collective-permute-start | bytes 442376 | tf_op jit(solution)/shard_map/ppermute | solution.py:15
  128.4 0.0 collective-permute-done.6
  128.4 0.9 fusion.18
  129.4 3.5 %collective-permute-done.7 = f32[1,2,144,128]{3,2,1,0:T(8,128)S(1)} collective-permute-done((f32[1,2,144,128]{3,2,1,0:T(8,128)}, f32[1,2,144,128]{3,2,1,0:T(8,128)S(1)}, u32[]{:S(2)}, u32[]{:S(2)}) %collective-permute-start.7) | collective-permute-done | bytes 147488 | tf_op jit(solution)/shard_map/ppermute | solution.py:15
  132.9 0.7 convert_element_type.13
  133.6 0.0 copy-done.1
  (9 shorter events, 0.2 us)
Async XLA Ops:
  0.6 5.3 %copy-start = (bf16[1,1,40,144,128]{4,3,2,1,0:T(8,128)(2,1)S(1)}, bf16[1,1,40,144,128]{4,3,2,1,0:T(8,128)(2,1)}, u32[]{:S(2)}) copy-start(bf16[1,1,40,144,128]{4,3,2,1,0:T(8,128)(2,1)} %param.14) | copy-start | bytes 4423684
  2.3 84.9 %collective-permute-start = (bf16[1,2,144,128]{3,2,1,0:T(8,128)(2,1)}, bf16[1,2,144,128]{3,2,1,0:T(8,128)(2,1)}, u32[]{:S(2)}, u32[]{:S(2)}) collective-permute-start(bf16[1,2,144,128]{3,2,1,0:T(8,128)(2,1)} %get-tuple-element.58), channel_id=1, source_target_pairs={{0,4},{4,8},{8,12},{12,16},{16,20},{20,24},{24,28},{28,0},{1,5},{5... | collective-permute-start | bytes 221192 | tf_op jit(solution)/shard_map/ppermute | solution.py:24
  3.8 84.4 %collective-permute-start.1 = (bf16[1,2,144,128]{3,2,1,0:T(8,128)(2,1)}, bf16[1,2,144,128]{3,2,1,0:T(8,128)(2,1)S(1)}, u32[]{:S(2)}, u32[]{:S(2)}) collective-permute-start(bf16[1,2,144,128]{3,2,1,0:T(8,128)(2,1)} %get-tuple-element.57), channel_id=1, source_target_pairs={{4,0},{8,4},{12,8},{16,12},{20,16},{24,20},{28,24},{0,28},{5,1},{9... | collective-permute-start | bytes 221192 | tf_op jit(solution)/shard_map/ppermute | solution.py:27
  5.9 23.1 %copy-start.4 = (s32[1,1,40,16]{2,3,1,0:T(8,128)S(1)}, s32[1,1,40,16]{2,3,1,0:T(8,128)}, u32[]{:S(2)}) copy-start(s32[1,1,40,16]{2,3,1,0:T(8,128)} %param.16) | copy-start | bytes 7684
  29.1 59.1 %copy-start.3 = (bf16[2,2,144,128]{3,2,1,0:T(8,128)(2,1)S(1)}, bf16[2,2,144,128]{3,2,1,0:T(8,128)(2,1)}, u32[]{:S(2)}) copy-start(bf16[2,2,144,128]{3,2,1,0:T(8,128)(2,1)} %param.13) | copy-start | bytes 442372
  29.1 80.2 %slice-start = ((s8[20971520]{0:T(1024)(128)(4,1)}), s8[4194304]{0:T(1024)(128)(4,1)S(1)}, s32[]{:S(2)}) async-start(s8[20971520]{0:T(1024)(128)(4,1)} %bitcast.57), calls=%async_computation | async-start | bytes 8388608
  29.1 80.2 %slice-start.1 = ((s8[20971520]{0:T(1024)(128)(4,1)}), s8[4194304]{0:T(1024)(128)(4,1)S(1)}, s32[]{:S(2)}) async-start(s8[20971520]{0:T(1024)(128)(4,1)} %bitcast.57), calls=%async_computation.1 | async-start | bytes 8388608
  29.1 80.2 %slice-start.2 = ((s8[20971520]{0:T(1024)(128)(4,1)}), s8[4194304]{0:T(1024)(128)(4,1)S(1)}, s32[]{:S(2)}) async-start(s8[20971520]{0:T(1024)(128)(4,1)} %bitcast.57), calls=%async_computation.2 | async-start | bytes 8388608
  88.3 4.8 %collective-permute-start.2 = (bf16[4,1,144,128]{3,2,1,0:T(8,128)(2,1)S(1)}, bf16[4,1,144,128]{3,2,1,0:T(8,128)(2,1)S(1)}, u32[]{:S(2)}, u32[]{:S(2)}) collective-permute-start(bf16[4,1,144,128]{3,2,1,0:T(8,128)(2,1)S(1)} %get-tuple-element.55), channel_id=1, source_target_pairs={{0,1},{1,2},{2,3},{3,0},{4,5},{5,6},{6,7},{7,4},{8,9},{9,10},{10,1... | collective-permute-start | bytes 442376 | tf_op jit(solution)/shard_map/ppermute | solution.py:24
  88.3 5.9 %collective-permute-start.3 = (bf16[4,1,144,128]{3,2,1,0:T(8,128)(2,1)S(1)}, bf16[4,1,144,128]{3,2,1,0:T(8,128)(2,1)S(1)}, u32[]{:S(2)}, u32[]{:S(2)}) collective-permute-start(bf16[4,1,144,128]{3,2,1,0:T(8,128)(2,1)S(1)} %get-tuple-element.56), channel_id=1, source_target_pairs={{1,0},{2,1},{3,2},{0,3},{5,4},{6,5},{7,6},{4,7},{9,8},{10,9},{11,1... | collective-permute-start | bytes 442376 | tf_op jit(solution)/shard_map/ppermute | solution.py:27
  90.7 18.7 %slice-start.3 = ((s8[20971520]{0:T(1024)(128)(4,1)}), s8[4194304]{0:T(1024)(128)(4,1)S(1)}, s32[]{:S(2)}) async-start(s8[20971520]{0:T(1024)(128)(4,1)} %bitcast.57), calls=%async_computation.3 | async-start | bytes 8388608
  90.7 14.3 %collective-permute-start.4 = (f32[4,1,144,128]{3,2,1,0:T(8,128)S(1)}, f32[4,1,144,128]{3,2,1,0:T(8,128)S(1)}, u32[]{:S(2)}, u32[]{:S(2)}) collective-permute-start(f32[4,1,144,128]{3,2,1,0:T(8,128)S(1)} %copy.20), channel_id=1, source_target_pairs={{0,1},{1,2},{2,3},{3,0},{4,5},{5,6},{6,7},{7,4},{8,9},{9,10},{10,1... | collective-permute-start | bytes 884744 | tf_op jit(solution)/shard_map/ppermute | solution.py:9
  90.8 14.3 %collective-permute-start.5 = (f32[4,1,144,128]{3,2,1,0:T(8,128)S(1)}, f32[4,1,144,128]{3,2,1,0:T(8,128)S(1)}, u32[]{:S(2)}, u32[]{:S(2)}) collective-permute-start(f32[4,1,144,128]{3,2,1,0:T(8,128)S(1)} %copy.21), channel_id=1, source_target_pairs={{0,3},{1,0},{2,1},{3,2},{4,7},{5,4},{6,5},{7,6},{8,11},{9,8},{10,9... | collective-permute-start | bytes 884744 | tf_op jit(solution)/shard_map/ppermute | solution.py:9
  94.3 15.1 %slice-start.4 = ((s8[20971520]{0:T(1024)(128)(4,1)}), s8[4194304]{0:T(1024)(128)(4,1)S(1)}, s32[]{:S(2)}) async-start(s8[20971520]{0:T(1024)(128)(4,1)} %bitcast.57), calls=%async_computation.4 | async-start | bytes 8388608
  105.1 0.8 copy-start.2
  106.7 26.9 %copy-start.1 = (bf16[1,1,40,144,128]{4,3,2,1,0:T(8,128)(2,1)S(1)}, bf16[1,1,40,144,128]{4,3,2,1,0:T(8,128)(2,1)}, u32[]{:S(2)}) copy-start(bf16[1,1,40,144,128]{4,3,2,1,0:T(8,128)(2,1)} %param.14) | copy-start | bytes 4423684
  106.7 21.7 %collective-permute-start.6 = (f32[1,2,144,128]{3,2,1,0:T(8,128)}, f32[1,2,144,128]{3,2,1,0:T(8,128)S(1)}, u32[]{:S(2)}, u32[]{:S(2)}) collective-permute-start(f32[1,2,144,128]{3,2,1,0:T(8,128)} %get-tuple-element.54), channel_id=1, source_target_pairs={{0,4},{4,8},{8,12},{12,16},{16,20},{20,24},{24,28},{1,5},{5,9},{9,... | collective-permute-start | bytes 442376 | tf_op jit(solution)/shard_map/ppermute | solution.py:15
  124.2 8.7 %collective-permute-start.7 = (f32[1,2,144,128]{3,2,1,0:T(8,128)}, f32[1,2,144,128]{3,2,1,0:T(8,128)S(1)}, u32[]{:S(2)}, u32[]{:S(2)}) collective-permute-start(f32[1,2,144,128]{3,2,1,0:T(8,128)} %get-tuple-element.53), channel_id=1, source_target_pairs={{4,0},{8,4},{12,8},{16,12},{20,16},{24,20},{28,24},{5,1},{9,5},{13... | collective-permute-start | bytes 442376 | tf_op jit(solution)/shard_map/ppermute | solution.py:15
where the time goes:
time: 136 us; the launch traced here: 134 us
  matrix products  106 us (78%)
  starting transfers between devices  13.4 us (10%)
  local copies, waits for them, and re-layouts  6.28 us (5%)
  waiting for transfers between devices  4.68 us (3%)
  other arithmetic  2.49 us (2%)
    dot_general x1, matrix products, body(): jnp.einsum('tke,tkws->ews', selector.astype(jnp.float32), contribution, p...  58.1 us
    dot_general x1, matrix products, body(): jnp.einsum('twb,tksb->tkws', cotan_local, blocks, preferred_element_type=...  23.1 us
    dot_general x1, matrix products, body(): jnp.einsum('tkws,tksb->twb', picked, blocks, preferred_element_type=jnp.f...  13.8 us
    dot_general x1, matrix products, body(): jnp.einsum('tke,ews->tkws', selector.astype(jnp.bfloat16), flattened, pre...  10.7 us
    ppermute x2, starting transfers between devices, passed_along(): return lax.ppermute(block, axis, route)  6.86 us
    ppermute x2, waiting for transfers between devices, passed_along(): return lax.ppermute(block, axis, route)  3.49 us
    ppermute x2, starting transfers between devices, with_halo(): lax.ppermute(lax.slice_in_dim(block, 0, width, axis=dim), axis, backward)  3.17 us
  transfers between devices with their start and end apart: 8, of which 2 were waited for; matrix products, arithmetic and copies ran while one was open for 83% of the time, Pallas kernels for 0%

commit v1 on v0

v1 whole, which is shorter than its diff:
```python
import functools

import jax
import jax.numpy as jnp
from jax import lax
from jax.experimental import pallas as pl
from jax.experimental.pallas import tpu as pltpu
from jax.sharding import PartitionSpec as P

GROUP = 4
WAYS = ((1, 1), (1, -1), (-1, 1), (-1, -1), (1, 0), (-1, 0), (0, 1), (0, -1))


def sent_span(by, side):
    return pl.ds(side - 1 if by > 0 else 0, 1 if by else side)


def held_span(by, side):
    return pl.ds(0 if by > 0 else (side + 1 if by < 0 else 1), 1 if by else side)


def greet(sizes):
    lats, lons = sizes
    lat, lon = lax.axis_index("lat"), lax.axis_index("lon")
    barrier = pltpu.get_barrier_semaphore()
    for i, j in WAYS:
        @pl.when((lat + i >= 0) & (lat + i < lats))
        def _(i=i, j=j):
            pl.semaphore_signal(
                barrier,
                inc=1,
                device_id=(lat + i, lax.rem(lon + j + lons, lons)),
                device_id_type=pl.DeviceIdType.MESH,
            )
    north = (lat > 0).astype(jnp.int32)
    south = (lat < lats - 1).astype(jnp.int32)
    pl.semaphore_wait(barrier, 2 + 3 * north + 3 * south)


def send_all(sizes, source, landing, send_sems, recv_sems):
    lats, lons = sizes
    lat, lon = lax.axis_index("lat"), lax.axis_index("lon")
    for way, (i, j) in enumerate(WAYS):
        @pl.when((lat + i >= 0) & (lat + i < lats))
        def _(way=way, i=i, j=j):
            pltpu.make_async_remote_copy(
                src_ref=source(i, j),
                dst_ref=landing(way, i, j),
                send_sem=send_sems.at[way],
                recv_sem=recv_sems.at[way],
                device_id=(lat + i, lax.rem(lon + j + lons, lons)),
                device_id_type=pl.DeviceIdType.MESH,
            ).start()


def await_way(sizes, source, landing, send_sems, recv_sems, way, then=None, otherwise=None):
    lats, lons = sizes
    lat, lon = lax.axis_index("lat"), lax.axis_index("lon")
    i, j = WAYS[way]
    copy = pltpu.make_async_remote_copy(
        src_ref=source(i, j),
        dst_ref=landing(way, i, j),
        send_sem=send_sems.at[way],
        recv_sem=recv_sems.at[way],
        device_id=(lat, lax.rem(lon + 1, lons)),
        device_id_type=pl.DeviceIdType.MESH,
    )

    @pl.when((lat - i >= 0) & (lat - i < lats))
    def _():
        copy.wait_recv()
        if then is not None:
            then()

    if otherwise is not None:
        @pl.when((lat - i < 0) | (lat - i >= lats))
        def _():
            otherwise()

    @pl.when((lat + i >= 0) & (lat + i < lats))
    def _():
        copy.wait_send()


def halo_kernel(sizes, own_ref, ext_ref, send_sems, recv_sems):
    side = own_ref.shape[0]

    def source(i, j):
        return own_ref.at[sent_span(i, side), sent_span(j, side)]

    def landing(way, i, j):
        return ext_ref.at[held_span(i, side), held_span(j, side)]

    greet(sizes)
    send_all(sizes, source, landing, send_sems, recv_sems)
    ext_ref[1:side + 1, 1:side + 1] = own_ref[...]
    for way, (i, j) in enumerate(WAYS):
        def clear(i=i, j=j):
            rows, cols = held_span(i, side), held_span(j, side)
            ext_ref[rows, cols] = jnp.zeros((rows.size, cols.size) + ext_ref.shape[2:], ext_ref.dtype)

        await_way(
            sizes, source, landing, send_sems, recv_sems, way, otherwise=clear if i else None
        )


def fold_kernel(sizes, part_ref, out_ref, *rest):
    acc, send_sems, recv_sems = rest[-3:]
    held = rest[:-3]
    side = out_ref.shape[0]

    def away(by):
        return pl.ds(side + 1 if by > 0 else (0 if by < 0 else 1), 1 if by else side)

    def source(i, j):
        return part_ref.at[away(i), away(j)]

    def landing(way, i, j):
        return held[way]

    greet(sizes)
    send_all(sizes, source, landing, send_sems, recv_sems)
    acc[...] = part_ref[1:side + 1, 1:side + 1]
    for way in reversed(range(len(WAYS))):
        i, j = WAYS[way]

        def add(way=way, i=i, j=j):
            rows = pl.ds(0 if i >= 0 else side - 1, 1 if i else side)
            cols = pl.ds(0 if j >= 0 else side - 1, 1 if j else side)
            acc[rows, cols] += held[way][...]

        await_way(sizes, source, landing, send_sems, recv_sems, way, then=add)
    out_ref[...] = acc[...].astype(out_ref.dtype)


def slot_place(ids_ref, t, k, live, side, lon_count):
    cycle = side * lon_count
    source = ids_ref[0, 0, t, k]
    row = lax.div(source, cycle)
    col = source - row * cycle
    ext_row = row - lax.axis_index("lat") * side + 1
    ext_col = col - lax.axis_index("lon") * side + 1
    ext_col = jnp.where(ext_col < 0, ext_col + cycle, ext_col)
    ext_col = jnp.where(ext_col >= cycle, ext_col - cycle, ext_col)
    width = side + 2
    return jnp.where(k < live, ext_row * width + ext_col, width * width)


def groups_of(live):
    return lax.div(live + (GROUP - 1), GROUP)


def weight_copy(w_ref, w_vmem, sems, t, g):
    return pltpu.make_async_copy(
        w_ref.at[0, 0, t, pl.ds(g * GROUP, GROUP)],
        w_vmem.at[t, pl.ds(g * GROUP, GROUP)],
        sems.at[t, g],
    )


def compute_kernel(
    side, lon_count, ids_ref, counts_ref, ext_ref, cot_ref, w_ref,
    ocean_ref, part_ref, ext, acc, w_vmem, sems,
):
    targets, slots = w_vmem.shape[:2]
    width = side + 2

    @pl.loop(0, targets)
    def _(t):
        groups = groups_of(counts_ref[0, 0, t])
        for g in range(slots // GROUP):
            @pl.when(g < groups)
            def _(g=g):
                weight_copy(w_ref, w_vmem, sems, t, g).start()

    ext[0:width * width] = ext_ref[...].reshape((width * width,) + ext.shape[1:])
    ext[width * width] = jnp.zeros(ext.shape[1:], ext.dtype)
    acc[...] = jnp.zeros_like(acc)

    def work(t, live, n):
        if n == 0:
            ocean_ref[0, 0, t] = jnp.zeros(ocean_ref.shape[3:], ocean_ref.dtype)
            return
        for g in range(n):
            weight_copy(w_ref, w_vmem, sems, t, g).wait()
        places = [slot_place(ids_ref, t, k, live, side, lon_count) for k in range(n * GROUP)]
        cot = cot_ref[0, 0, t]
        picked = jnp.concatenate([ext[p] for p in places], axis=1)
        blocks = w_vmem[t, 0:n * GROUP]
        blocks = blocks.reshape(blocks.shape[0] * blocks.shape[1], blocks.shape[2])
        total = jnp.dot(picked, blocks, preferred_element_type=jnp.float32)
        ocean_ref[0, 0, t] = total.astype(ocean_ref.dtype)
        cells = w_vmem.shape[2]
        for k in range(0, n * GROUP, 2):
            both = lax.dot_general(
                cot,
                blocks[k * cells:(k + 2) * cells],
                (((1,), (1,)), ((), ())),
                preferred_element_type=jnp.float32,
            )
            for m in range(2):
                acc[places[k + m]] += both[:, m * cells:(m + 1) * cells]

    @pl.loop(0, targets)
    def _(t):
        live = counts_ref[0, 0, t]
        groups = groups_of(live)
        for n in range(slots // GROUP + 1):
            @pl.when(groups == n)
            def _(n=n):
                work(t, live, n)

    part_ref[...] = acc[0:width * width].reshape(part_ref.shape)


def compute(side, lon_count, source_ids, counts, ext, cotangent, weights):
    smem = pl.BlockSpec(memory_space=pltpu.SMEM)
    vmem = pl.BlockSpec(memory_space=pltpu.VMEM)
    hbm = pl.BlockSpec(memory_space=pl.ANY)
    targets, slots = weights.shape[2:4]
    width, tail = side + 2, ext.shape[2:]
    flops = 4 * targets * slots * tail[0] * tail[1] * tail[1]
    return pl.pallas_call(
        functools.partial(compute_kernel, side, lon_count),
        out_shape=[
            jax.ShapeDtypeStruct(cotangent.shape, jnp.bfloat16),
            jax.ShapeDtypeStruct(ext.shape, jnp.float32),
        ],
        in_specs=[smem, smem, vmem, vmem, hbm],
        out_specs=[vmem, vmem],
        scratch_shapes=[
            pltpu.VMEM((width * width + 1,) + tail, ext.dtype),
            pltpu.VMEM((width * width + 1,) + tail, jnp.float32),
            pltpu.VMEM(weights.shape[2:], weights.dtype),
            pltpu.SemaphoreType.DMA((targets, slots // GROUP)),
        ],
        compiler_params=pltpu.CompilerParams(vmem_limit_bytes=48 * 1024 * 1024),
        cost_estimate=pl.CostEstimate(
            flops=flops, bytes_accessed=weights.size * 2, transcendentals=0
        ),
        name="products",
    )(source_ids, counts, ext, cotangent, weights)


def body(increment, cotangent, weights, source_ids, counts):
    side, _, levels, cells = increment.shape
    sizes = lax.axis_size("lat"), lax.axis_size("lon")
    vmem = pl.BlockSpec(memory_space=pltpu.VMEM)
    ways = len(WAYS)
    wide = (side + 2, side + 2, levels, cells)
    sems = [pltpu.SemaphoreType.DMA((ways,)), pltpu.SemaphoreType.DMA((ways,))]
    ext = pl.pallas_call(
        functools.partial(halo_kernel, sizes),
        out_shape=jax.ShapeDtypeStruct(wide, increment.dtype),
        in_specs=[vmem],
        out_specs=vmem,
        scratch_shapes=sems,
        compiler_params=pltpu.CompilerParams(collective_id=0, has_side_effects=True),
        name="halo",
    )(increment)
    ocean, part = compute(side, sizes[1], source_ids, counts, ext, cotangent, weights)
    landings = [
        pltpu.VMEM((1 if i else side, 1 if j else side, levels, cells), jnp.float32)
        for i, j in WAYS
    ]
    folded = pl.pallas_call(
        functools.partial(fold_kernel, sizes),
        out_shape=jax.ShapeDtypeStruct(increment.shape, jnp.bfloat16),
        in_specs=[vmem],
        out_specs=vmem,
        scratch_shapes=landings + [pltpu.VMEM(increment.shape, jnp.float32)] + sems,
        compiler_params=pltpu.CompilerParams(collective_id=1, has_side_effects=True),
        name="fold",
    )(part)
    return ocean, folded


def solution(mesh):
    placed = (
        P("lat", "lon", None, None),
        P("lat", "lon", None, None, None),
        P("lat", "lon", None, None, None, None),
        P("lat", "lon", None, None),
        P("lat", "lon", None),
    )
    return jax.shard_map(
        body,
        mesh=mesh,
        in_specs=placed,
        out_specs=(P("lat", "lon", None, None, None), P("lat", "lon", None, None)),
        check_vma=False,
    )
```

time: 136 us -> 59.5 us (0.44); the launches traced: 134 us -> 59.1 us
  matrix products: 106 us -> 0 us
  Pallas kernels: 0 us -> 52 us
  starting transfers between devices: 13.4 us -> 0 us
  waiting for transfers between devices: 4.68 us -> 0 us
  other arithmetic: 2.49 us -> 0 us
    dot_general x4 -> x0, matrix products: 106 us -> none  [the longest x1 58.1 us: body(): jnp.einsum('tke,tkws->ews', selector.astype(jnp.float32), contribution, p...]
    pallas_call x0 -> x3, Pallas kernels: none -> 52 us  [the longest x1 20.6 us: compute(): pl.pallas_call(functools.partial(compute_kernel, side, lon_count), out_sh...]
    ppermute x8 -> x0, starting transfers between devices: 13.4 us -> none  [the longest x2 6.86 us: passed_along(): return lax.ppermute(block, axis, route)]
    ppermute x8 -> x0, waiting for transfers between devices: 4.68 us -> none  [the longest x2 3.49 us: passed_along(): return lax.ppermute(block, axis, route)]
    unnamed x25 -> x10, local copies, waits for them, and re-layouts: 1.93 us -> 6.45 us
    slice x6 -> x0, local copies, waits for them, and re-layouts: 4.33 us -> none  [the longest x1 1.7 us: with_halo(): lax.slice_in_dim(block, 0, width, axis=dim)]
  transfers between devices with their start and end apart: 8 -> 0, of which waited for: 2 -> 0; matrix products, arithmetic and copies ran while one was open for 83% -> 0% of each run, Pallas kernels for 0% -> 0%
where the time goes in v1:
time: 59.5 us; the launch traced here: 59.1 us
  Pallas kernels  52 us (87%)
  local copies, waits for them, and re-layouts  6.45 us (11%)
  between operations  0.67 us (1%)
    pallas_call x1, Pallas kernels, compute(): pl.pallas_call(functools.partial(compute_kernel, side, lon_count), out_sh...  20.6 us
    pallas_call x1, Pallas kernels, body(): pl.pallas_call(functools.partial(fold_kernel, sizes), out_shape=jax.Shape...  18.3 us
    pallas_call x1, Pallas kernels, body(): pl.pallas_call(functools.partial(halo_kernel, sizes), out_shape=jax.Shape...  13 us
    unnamed x10, local copies, waits for them, and re-layouts  6.45 us

profile of v1, /device:TPU:8, one launch (start us, length us, event | category | flops | bytes accessed | tf_op | source)
XLA Modules:
  0.0 59.1 jit_solution(1757418722107430876)
XLA Ops:
  0.6 0.8 %copy.7.ids_ref = s32[1,1,40,16]{3,2,1,0:T(8,128)S(1)} copy(s32[1,1,40,16]{2,3,1,0:T(8,128)} %param.8) | data formatting | bytes 5120 | tf_op args[3]
  1.4 13.0 %halo.1.ext_ref = bf16[4,4,144,128]{3,2,1,0:T(8,128)(2,1)} custom-call(bf16[2,2,144,128]{3,2,1,0:T(8,128)(2,1)} %own_ref.1), custom_call_target="tpu_custom_call" | custom-call | tf_op jit(solution)/shard_map/halo/pallas_call | solution.py:252
  14.5 0.0 copy-start
  14.5 1.1 %copy-done = bf16[4,4,144,128]{3,2,1,0:T(8,128)(2,1)S(1)} copy-done((bf16[4,4,144,128]{3,2,1,0:T(8,128)(2,1)S(1)}, bf16[4,4,144,128]{3,2,1,0:T(8,128)(2,1)}, u32[]{:S(2)}) %copy-start) | copy-done | bytes 589848
  15.5 0.0 copy-start.1
  15.5 1.4 %copy-done.1 = bf16[1,1,40,144,128]{4,3,2,1,0:T(8,128)(2,1)S(1)} copy-done((bf16[1,1,40,144,128]{4,3,2,1,0:T(8,128)(2,1)S(1)}, bf16[1,1,40,144,128]{4,3,2,1,0:T(8,128)(2,1)}, u32[]{:S(2)}) %copy-start.1) | copy-done | bytes 1474584
  16.9 0.0 copy-start.3
  16.9 0.7 %copy-done.3 = s32[1,1,40]{2,1,0:T(1,128)S(1)} copy-done((s32[1,1,40]{2,1,0:T(1,128)S(1)}, s32[1,1,40]{2,1,0:T(1,128)}, u32[]{:S(2)}) %copy-start.3) | copy-done | bytes 184
  17.6 20.6 %products.1 = (bf16[1,1,40,144,128]{4,3,2,1,0:T(8,128)(2,1)}, f32[4,4,144,128]{3,2,1,0:T(8,128)S(1)}) custom-call(s32[1,1,40,16]{3,2,1,0:T(8,128)S(1)} %copy.7.ids_ref, s32[1,1,40]{2,1,0:T(1,128)S(1)} %copy-done.3, bf16[4,4,144,128]{3,2,1,0:T(8,128)(2,1)S(1)} %copy-done, bf16[1,1,40,144,128]{4,3,2,1,0:T(8,128)(2,1)S(1)} %copy-done.1, ...), custom_call_target="tpu_custom_call" | custom-call | flops 6039797760 | bytes 20971520 | tf_op jit(solution)/shard_map/products/pallas_call | solution.py:223
  38.2 0.0 copy-start.2
  38.2 1.0 %copy-done.2 = f32[4,4,144,128]{3,2,1,0:T(8,128)} copy-done((f32[4,4,144,128]{3,2,1,0:T(8,128)}, f32[4,4,144,128]{3,2,1,0:T(8,128)S(1)}, u32[]{:S(2)}) %copy-start.2) | copy-done | bytes 1179672
  39.2 18.3 %fold.1 = bf16[2,2,144,128]{3,2,1,0:T(8,128)(2,1)} custom-call(f32[4,4,144,128]{3,2,1,0:T(8,128)} %copy-done.2), custom_call_target="tpu_custom_call" | custom-call | tf_op jit(solution)/shard_map/fold/pallas_call | solution.py:266
  57.5 1.6 %copy.9 = bf16[2,2,144,128]{3,2,1,0:T(8,128)(2,1)} copy(bf16[2,2,144,128]{3,2,1,0:T(8,128)(2,1)} %fold.1) | data formatting | bytes 294912
Async XLA Ops:
  14.5 1.1 %copy-start = (bf16[4,4,144,128]{3,2,1,0:T(8,128)(2,1)S(1)}, bf16[4,4,144,128]{3,2,1,0:T(8,128)(2,1)}, u32[]{:S(2)}) copy-start(bf16[4,4,144,128]{3,2,1,0:T(8,128)(2,1)} %halo.1.ext_ref) | copy-start | bytes 1769476
  15.5 1.4 %copy-start.1 = (bf16[1,1,40,144,128]{4,3,2,1,0:T(8,128)(2,1)S(1)}, bf16[1,1,40,144,128]{4,3,2,1,0:T(8,128)(2,1)}, u32[]{:S(2)}) copy-start(bf16[1,1,40,144,128]{4,3,2,1,0:T(8,128)(2,1)} %cot_ref.1) | copy-start | bytes 4423684
  16.9 0.7 %copy-start.3 = (s32[1,1,40]{2,1,0:T(1,128)S(1)}, s32[1,1,40]{2,1,0:T(1,128)}, u32[]{:S(2)}) copy-start(s32[1,1,40]{2,1,0:T(1,128)} %counts_ref.1) | copy-start | bytes 484
  38.2 1.0 %copy-start.2 = (f32[4,4,144,128]{3,2,1,0:T(8,128)}, f32[4,4,144,128]{3,2,1,0:T(8,128)S(1)}, u32[]{:S(2)}) copy-start(f32[4,4,144,128]{3,2,1,0:T(8,128)S(1)} %get-tuple-element.5.part_ref) | copy-start | bytes 3538948

commit v2 on v1

v2 whole, which is shorter than its diff:
```python
import functools

import jax
import jax.numpy as jnp
from jax import lax
from jax.experimental import pallas as pl
from jax.experimental.pallas import tpu as pltpu
from jax.sharding import PartitionSpec as P

GROUP = 4
WAYS = ((1, 1), (1, -1), (-1, 1), (-1, -1), (1, 0), (-1, 0), (0, 1), (0, -1))


def sent_span(by, side):
    return pl.ds(side - 1 if by > 0 else 0, 1 if by else side)


def held_span(by, side):
    return pl.ds(0 if by > 0 else (side + 1 if by < 0 else 1), 1 if by else side)


def greet(sizes):
    lats, lons = sizes
    lat, lon = lax.axis_index("lat"), lax.axis_index("lon")
    barrier = pltpu.get_barrier_semaphore()
    for i, j in WAYS:
        @pl.when((lat + i >= 0) & (lat + i < lats))
        def _(i=i, j=j):
            pl.semaphore_signal(
                barrier,
                inc=1,
                device_id=(lat + i, lax.rem(lon + j + lons, lons)),
                device_id_type=pl.DeviceIdType.MESH,
            )
    north = (lat > 0).astype(jnp.int32)
    south = (lat < lats - 1).astype(jnp.int32)
    pl.semaphore_wait(barrier, 2 + 3 * north + 3 * south)


def send_all(sizes, source, landing, send_sems, recv_sems):
    lats, lons = sizes
    lat, lon = lax.axis_index("lat"), lax.axis_index("lon")
    for way, (i, j) in enumerate(WAYS):
        @pl.when((lat + i >= 0) & (lat + i < lats))
        def _(way=way, i=i, j=j):
            pltpu.make_async_remote_copy(
                src_ref=source(i, j),
                dst_ref=landing(way, i, j),
                send_sem=send_sems.at[way],
                recv_sem=recv_sems.at[way],
                device_id=(lat + i, lax.rem(lon + j + lons, lons)),
                device_id_type=pl.DeviceIdType.MESH,
            ).start()


def await_way(sizes, source, landing, send_sems, recv_sems, way, then=None, otherwise=None):
    lats, lons = sizes
    lat, lon = lax.axis_index("lat"), lax.axis_index("lon")
    i, j = WAYS[way]
    copy = pltpu.make_async_remote_copy(
        src_ref=source(i, j),
        dst_ref=landing(way, i, j),
        send_sem=send_sems.at[way],
        recv_sem=recv_sems.at[way],
        device_id=(lat, lax.rem(lon + 1, lons)),
        device_id_type=pl.DeviceIdType.MESH,
    )

    @pl.when((lat - i >= 0) & (lat - i < lats))
    def _():
        copy.wait_recv()
        if then is not None:
            then()

    if otherwise is not None:
        @pl.when((lat - i < 0) | (lat - i >= lats))
        def _():
            otherwise()

    @pl.when((lat + i >= 0) & (lat + i < lats))
    def _():
        copy.wait_send()


def slot_place(ids_ref, t, k, live, side, lon_count):
    cycle = side * lon_count
    source = ids_ref[0, 0, t, k]
    row = lax.div(source, cycle)
    col = source - row * cycle
    ext_row = row - lax.axis_index("lat") * side + 1
    ext_col = col - lax.axis_index("lon") * side + 1
    ext_col = jnp.where(ext_col < 0, ext_col + cycle, ext_col)
    ext_col = jnp.where(ext_col >= cycle, ext_col - cycle, ext_col)
    width = side + 2
    return jnp.where(k < live, ext_row * width + ext_col, width * width)


def groups_of(live):
    return lax.div(live + (GROUP - 1), GROUP)


def weight_copy(w_ref, w_vmem, sems, t, g):
    return pltpu.make_async_copy(
        w_ref.at[0, 0, t, pl.ds(g * GROUP, GROUP)],
        w_vmem.at[t, pl.ds(g * GROUP, GROUP)],
        sems.at[t, g],
    )


def adjoint_kernel(
    side, lon_count, ids_ref, counts_ref, cot_ref, w_ref, part_ref, acc, w_vmem, sems
):
    targets, slots = w_vmem.shape[:2]
    width = side + 2

    @pl.loop(0, targets)
    def _(t):
        groups = groups_of(counts_ref[0, 0, t])
        for g in range(slots // GROUP):
            @pl.when(g < groups)
            def _(g=g):
                weight_copy(w_ref, w_vmem, sems, t, g).start()

    acc[...] = jnp.zeros_like(acc)

    def work(t, live, n):
        for g in range(n):
            weight_copy(w_ref, w_vmem, sems, t, g).wait()
        places = [slot_place(ids_ref, t, k, live, side, lon_count) for k in range(n * GROUP)]
        cot = cot_ref[0, 0, t]
        cells = w_vmem.shape[2]
        for k in range(0, n * GROUP, 2):
            pair = w_vmem[t, k:k + 2].reshape(2 * cells, w_vmem.shape[3])
            both = lax.dot_general(
                cot, pair, (((1,), (1,)), ((), ())), preferred_element_type=jnp.float32
            )
            for m in range(2):
                acc[places[k + m]] += both[:, m * cells:(m + 1) * cells]

    @pl.loop(0, targets)
    def _(t):
        live = counts_ref[0, 0, t]
        groups = groups_of(live)
        for n in range(1, slots // GROUP + 1):
            @pl.when(groups == n)
            def _(n=n):
                work(t, live, n)

    part_ref[...] = acc[0:width * width].reshape(part_ref.shape)


def exchange_kernel(
    sizes, ids_ref, counts_ref, own_ref, part_ref, w_ref, ocean_ref, out_ref, *rest
):
    ways = len(WAYS)
    held = rest[:ways]
    acc, halo, ext, w_vmem, w_sems, halo_send, halo_recv, fold_send, fold_recv = rest[ways:]
    side = out_ref.shape[0]
    width = side + 2
    targets, slots = w_vmem.shape[:2]

    def weights_of(t):
        return pltpu.make_async_copy(w_ref.at[0, 0, t], w_vmem.at[t], w_sems.at[t])

    @pl.loop(0, targets)
    def _(t):
        weights_of(t).start()

    def own_edge(i, j):
        return own_ref.at[sent_span(i, side), sent_span(j, side)]

    def halo_slot(way, i, j):
        return halo.at[held_span(i, side), held_span(j, side)]

    def away(by):
        return pl.ds(side + 1 if by > 0 else (0 if by < 0 else 1), 1 if by else side)

    def part_edge(i, j):
        return part_ref.at[away(i), away(j)]

    def fold_slot(way, i, j):
        return held[way]

    greet(sizes)
    send_all(sizes, own_edge, halo_slot, halo_send, halo_recv)
    send_all(sizes, part_edge, fold_slot, fold_send, fold_recv)
    halo[1:side + 1, 1:side + 1] = own_ref[...]
    ext[width * width] = jnp.zeros(ext.shape[1:], ext.dtype)
    acc[...] = part_ref[1:side + 1, 1:side + 1]
    for way, (i, j) in enumerate(WAYS):
        def clear(i=i, j=j):
            rows, cols = held_span(i, side), held_span(j, side)
            halo[rows, cols] = jnp.zeros((rows.size, cols.size) + halo.shape[2:], halo.dtype)

        await_way(
            sizes, own_edge, halo_slot, halo_send, halo_recv, way, otherwise=clear if i else None
        )
    ext[0:width * width] = halo[...].reshape((width * width,) + ext.shape[1:])

    @pl.loop(0, targets)
    def _(t):
        weights_of(t).wait()
        live = counts_ref[0, 0, t]
        picked = jnp.concatenate(
            [ext[slot_place(ids_ref, t, k, live, side, sizes[1])] for k in range(slots)], axis=1
        )
        blocks = w_vmem[t].reshape(slots * w_vmem.shape[2], w_vmem.shape[3])
        total = jnp.dot(picked, blocks, preferred_element_type=jnp.float32)
        ocean_ref[0, 0, t] = total.astype(ocean_ref.dtype)

    for way in reversed(range(ways)):
        i, j = WAYS[way]

        def add(way=way, i=i, j=j):
            rows = pl.ds(0 if i >= 0 else side - 1, 1 if i else side)
            cols = pl.ds(0 if j >= 0 else side - 1, 1 if j else side)
            acc[rows, cols] += held[way][...]

        await_way(sizes, part_edge, fold_slot, fold_send, fold_recv, way, then=add)
    out_ref[...] = acc[...].astype(out_ref.dtype)


def body(increment, cotangent, weights, source_ids, counts):
    side, _, levels, cells = increment.shape
    sizes = lax.axis_size("lat"), lax.axis_size("lon")
    smem = pl.BlockSpec(memory_space=pltpu.SMEM)
    vmem = pl.BlockSpec(memory_space=pltpu.VMEM)
    hbm = pl.BlockSpec(memory_space=pl.ANY)
    targets, slots = weights.shape[2:4]
    ways, width = len(WAYS), side + 2
    wide = (width, width, levels, cells)
    flat = (width * width + 1, levels, cells)
    cost = pl.CostEstimate(
        flops=2 * targets * slots * levels * cells * cells,
        bytes_accessed=weights.size * 2,
        transcendentals=0,
    )
    limit = 48 * 1024 * 1024
    part = pl.pallas_call(
        functools.partial(adjoint_kernel, side, sizes[1]),
        out_shape=jax.ShapeDtypeStruct(wide, jnp.float32),
        in_specs=[smem, smem, vmem, hbm],
        out_specs=vmem,
        scratch_shapes=[
            pltpu.VMEM(flat, jnp.float32),
            pltpu.VMEM(weights.shape[2:], weights.dtype),
            pltpu.SemaphoreType.DMA((targets, slots // GROUP)),
        ],
        compiler_params=pltpu.CompilerParams(vmem_limit_bytes=limit),
        cost_estimate=cost,
        name="adjoint",
    )(source_ids, counts, cotangent, weights)
    landings = [
        pltpu.VMEM((1 if i else side, 1 if j else side, levels, cells), jnp.float32)
        for i, j in WAYS
    ]
    return pl.pallas_call(
        functools.partial(exchange_kernel, sizes),
        out_shape=[
            jax.ShapeDtypeStruct(cotangent.shape, jnp.bfloat16),
            jax.ShapeDtypeStruct(increment.shape, jnp.bfloat16),
        ],
        in_specs=[smem, smem, vmem, vmem, hbm],
        out_specs=[vmem, vmem],
        scratch_shapes=landings + [
            pltpu.VMEM(increment.shape, jnp.float32),
            pltpu.VMEM(wide, increment.dtype),
            pltpu.VMEM(flat, increment.dtype),
            pltpu.VMEM(weights.shape[2:], weights.dtype),
            pltpu.SemaphoreType.DMA((targets,)),
        ] + [pltpu.SemaphoreType.DMA((ways,))] * 4,
        compiler_params=pltpu.CompilerParams(
            collective_id=0, has_side_effects=True, vmem_limit_bytes=limit
        ),
        cost_estimate=cost,
        name="exchange",
    )(source_ids, counts, increment, part, weights)


def solution(mesh):
    placed = (
        P("lat", "lon", None, None),
        P("lat", "lon", None, None, None),
        P("lat", "lon", None, None, None, None),
        P("lat", "lon", None, None),
        P("lat", "lon", None),
    )
    return jax.shard_map(
        body,
        mesh=mesh,
        in_specs=placed,
        out_specs=(P("lat", "lon", None, None, None), P("lat", "lon", None, None)),
        check_vma=False,
    )
```

time: 59.5 us -> 53.3 us (0.90)
  Pallas kernels: 52 us -> 47.1 us
  local copies, waits for them, and re-layouts: 6.45 us -> 4.58 us
    pallas_call x3 -> x2, Pallas kernels: 52 us -> 47.1 us  [the longest x1 31.8 us: body(): pl.pallas_call(functools.partial(exchange_kernel, sizes), out_shape=[jax....]
    unnamed x10 -> x9, local copies, waits for them, and re-layouts: 6.45 us -> 4.58 us
where the time goes in v2:
time: 53.3 us; the launch traced here: 52.3 us
  Pallas kernels  47.1 us (88%)
  local copies, waits for them, and re-layouts  4.58 us (9%)
  between operations  0.66 us (1%)
    pallas_call x1, Pallas kernels, body(): pl.pallas_call(functools.partial(exchange_kernel, sizes), out_shape=[jax....  31.8 us
    pallas_call x1, Pallas kernels, body(): pl.pallas_call(functools.partial(adjoint_kernel, side, sizes[1]), out_sha...  15.3 us
    unnamed x9, local copies, waits for them, and re-layouts  4.58 us

profile of v2, /device:TPU:8, one launch (start us, length us, event | category | flops | bytes accessed | tf_op | source)
XLA Modules:
  0.0 52.3 jit_solution(13122744444087415262)
XLA Ops:
  0.6 0.8 %copy.8.ids_ref = s32[1,1,40,16]{3,2,1,0:T(8,128)S(1)} copy(s32[1,1,40,16]{2,3,1,0:T(8,128)} %param.8) | data formatting | bytes 5120 | tf_op args[3]
  1.4 0.0 copy-start
  1.4 1.4 %copy-done = bf16[1,1,40,144,128]{4,3,2,1,0:T(8,128)(2,1)S(1)} copy-done((bf16[1,1,40,144,128]{4,3,2,1,0:T(8,128)(2,1)S(1)}, bf16[1,1,40,144,128]{4,3,2,1,0:T(8,128)(2,1)}, u32[]{:S(2)}) %copy-start) | copy-done | bytes 1474584
  2.8 0.0 copy-start.2
  2.8 0.7 %copy-done.2 = s32[1,1,40]{2,1,0:T(1,128)S(1)} copy-done((s32[1,1,40]{2,1,0:T(1,128)S(1)}, s32[1,1,40]{2,1,0:T(1,128)}, u32[]{:S(2)}) %copy-start.2) | copy-done | bytes 184
  3.4 0.0 copy-start.1
  3.4 15.3 %adjoint.1.part_ref = f32[4,4,144,128]{3,2,1,0:T(8,128)S(1)} custom-call(s32[1,1,40,16]{3,2,1,0:T(8,128)S(1)} %copy.8.ids_ref, s32[1,1,40]{2,1,0:T(1,128)S(1)} %copy-done.2, bf16[1,1,40,144,128]{4,3,2,1,0:T(8,128)(2,1)S(1)} %copy-done, bf16[1,1,40,16,128,128]{5,4,3,2,1,0:T(8,128)(2,1)} %w_ref.3), custom_call_target="tpu_custom_call" | custom-call | flops 3019898880 | bytes 20971520 | tf_op jit(solution)/shard_map/adjoint/pallas_call | solution.py:239
  18.7 0.0 copy-done.1
  18.8 31.8 %exchange.1 = (bf16[1,1,40,144,128]{4,3,2,1,0:T(8,128)(2,1)S(1)}, bf16[2,2,144,128]{3,2,1,0:T(8,128)(2,1)S(1)}) custom-call(s32[1,1,40,16]{3,2,1,0:T(8,128)S(1)} %copy.8.ids_ref, s32[1,1,40]{2,1,0:T(1,128)S(1)} %copy-done.2, bf16[2,2,144,128]{3,2,1,0:T(8,128)(2,1)S(1)} %copy-done.1, f32[4,4,144,128]{3,2,1,0:T(8,128)S(1)} %adjoint.1.part_ref, ...), custom_call_target="tpu_custom_call" | custom-call | flops 3019898880 | bytes 20971520 | tf_op jit(solution)/shard_map/exchange/pallas_call | solution.py:257
  50.5 1.1 %copy.11 = bf16[1,1,40,144,128]{4,3,2,1,0:T(8,128)(2,1)} copy(bf16[1,1,40,144,128]{4,3,2,1,0:T(8,128)(2,1)S(1)} %get-tuple-element.4) | data formatting | bytes 2949120
  51.6 0.7 %copy.12 = bf16[2,2,144,128]{3,2,1,0:T(8,128)(2,1)} copy(bf16[2,2,144,128]{3,2,1,0:T(8,128)(2,1)S(1)} %get-tuple-element.5) | data formatting | bytes 294912
Async XLA Ops:
  1.4 1.4 %copy-start = (bf16[1,1,40,144,128]{4,3,2,1,0:T(8,128)(2,1)S(1)}, bf16[1,1,40,144,128]{4,3,2,1,0:T(8,128)(2,1)}, u32[]{:S(2)}) copy-start(bf16[1,1,40,144,128]{4,3,2,1,0:T(8,128)(2,1)} %cot_ref.1) | copy-start | bytes 4423684
  2.8 0.7 %copy-start.2 = (s32[1,1,40]{2,1,0:T(1,128)S(1)}, s32[1,1,40]{2,1,0:T(1,128)}, u32[]{:S(2)}) copy-start(s32[1,1,40]{2,1,0:T(1,128)} %counts_ref.3) | copy-start | bytes 484
  3.4 15.3 %copy-start.1 = (bf16[2,2,144,128]{3,2,1,0:T(8,128)(2,1)S(1)}, bf16[2,2,144,128]{3,2,1,0:T(8,128)(2,1)}, u32[]{:S(2)}) copy-start(bf16[2,2,144,128]{3,2,1,0:T(8,128)(2,1)} %own_ref.1) | copy-start | bytes 442372
